TPU v7x, 32 devices: a whole 2x2x4 slice. The times are simulated.
32 devices in a mesh: grp: 8 (over z, y), lane: 4 (over x, core).
Axes of the slice: x: 2, y: 2, z: 4, core: 2. Of those that a mesh axis runs over, the one named last changes fastest.
Arguments:
- grad_pooled: bfloat16 [4096, 16, 256], P(('grp', 'lane')), may hold values from -16 to 16
- bag_len: int32 [4096, 16], P(('grp', 'lane')), may hold values from 1 to 8
- lookup_slot: int32 [4096, 16, 8], P('grp', 'lane'), may hold values from -1 to 15, as said below
- slot_row: int32 [8, 4, 8, 2], P('grp', 'lane'), may hold values from 0 to 1023, as said below
- weights: float32 [16, 2048, 256], P('lane', 'grp'), may hold values from -6 to 6
- accum: float32 [16, 2048], P('lane', 'grp'), may hold values from 0.05 to 0.5
Outputs:
- new_weights: float32 [16, 2048, 256], P('lane', 'grp')
- new_accum: float32 [16, 2048], P('lane', 'grp')
Inputs may be any that keep to these rules, and one draw needn't show every extreme that they name: `lookup_slot`: position j of bag (b, t) holds -1 when j >= bag_len[b, t] and otherwise a slot number s; the row slot_row[s // 2, t // 4, g, s % 2], with g the group of sample b, lies in local table t % 4. `slot_row`: several slots, also from different groups, may name the same row.
All inputs are finite; a program needn't handle non-finite values.
Results may differ from a plain program's by a relative error of at most 0.0035.
Values may be sent and summed in bfloat16 or wider, within the bound.
A program may use at most 64 MiB of HBM per device.

v0:
```python
import math
import jax
import jax.numpy as jnp
from jax import lax
from jax.sharding import PartitionSpec as P

SLOTS_PEER = 2
LEARN_RATE = 0.3
EPSILON = 1e-06


def per_device(grad_pooled, bag_len, lookup_slot, slot_row, weights, accum):
    lane_count = lax.axis_size("lane")
    group_count = lax.axis_size("grp")
    number_slots = group_count * SLOTS_PEER
    batch_rows, table_count, embed_width = grad_pooled.shape
    tables_here = table_count // lane_count
    bag_depth = lookup_slot.shape[2]
    scaled = (grad_pooled.astype(jnp.float32) / bag_len.astype(jnp.float32)[:, :, None]).astype(
        jnp.bfloat16
    )
    own_slots = lax.all_to_all(lookup_slot, "lane", split_axis=0, concat_axis=1, tiled=True)
    slot_marks = jnp.transpose(
        own_slots.reshape(batch_rows, lane_count, tables_here, bag_depth), (1, 0, 2, 3)
    )
    numbers = lax.broadcasted_iota(jnp.int32, (1, number_slots, 1, 1, 1), 1)
    counts = jnp.sum(slot_marks[:, None] == numbers, axis=-1, dtype=jnp.int32).astype(jnp.bfloat16)
    values = scaled.reshape(batch_rows, lane_count, tables_here, embed_width)
    partial_here = jnp.einsum(
        "msbt,bmte->mse", counts, values, preferred_element_type=jnp.float32
    ).astype(jnp.bfloat16)
    partial_value = lax.all_to_all(partial_here, "lane", split_axis=0, concat_axis=0, tiled=True)
    slot_sum = jnp.sum(partial_value.astype(jnp.float32), axis=0).astype(jnp.bfloat16)
    outgoing = slot_sum.reshape(group_count, SLOTS_PEER, embed_width)
    incoming = lax.all_to_all(outgoing, "grp", split_axis=0, concat_axis=0, tiled=True).reshape(
        number_slots, embed_width
    )
    targets = slot_row.reshape(1, number_slots)
    local_rows = accum.shape[0] * accum.shape[1]
    row_ids = lax.broadcasted_iota(jnp.int32, (local_rows, 1), 0)
    placing = (row_ids == targets).astype(jnp.bfloat16)
    row_grad = jnp.dot(placing, incoming, preferred_element_type=jnp.float32)
    square_mean = jnp.mean(row_grad * row_grad, axis=1)
    norm_total = lax.psum(embed_width * jnp.sum(square_mean), ("grp", "lane"))
    clip_limit = 0.5 * math.sqrt(group_count * lane_count * number_slots * embed_width)
    clip_factor = clip_limit / jnp.maximum(jnp.sqrt(norm_total), clip_limit)
    new_accum = accum + clip_factor * clip_factor * square_mean.reshape(accum.shape)
    step_rows = LEARN_RATE * clip_factor * row_grad.reshape(weights.shape)
    new_weights = weights - step_rows / (jnp.sqrt(new_accum)[:, :, None] + EPSILON)
    return (new_weights, new_accum)


def solution(mesh):
    placed = (
        P(("grp", "lane"), None, None),
        P(("grp", "lane"), None),
        P("grp", "lane", None),
        P("grp", "lane", None, None),
        P("lane", "grp", None),
        P("lane", "grp"),
    )
    return jax.shard_map(
        per_device,
        mesh=mesh,
        in_specs=placed,
        out_specs=(P("lane", "grp", None), P("lane", "grp")),
        check_vma=False,
    )
```

profile of v0, /device:TPU:0, one launch (start us, length us, event | category | flops | bytes accessed | tf_op | source)
XLA Modules:
  0.0 79.0 jit_solution(7309163360748396572)
XLA Ops:
  0.6 0.0 copy-start.2
  0.6 0.0 copy-start
  0.6 1.3 %copy.21 = s32[512,4,8]{2,1,0:T(4,128)S(1)} copy(s32[512,4,8]{0,2,1:T(8,128)} %param.8) | data formatting | bytes 131072 | tf_op args[2]
  2.0 1.8 %reshape.32 = s32[4,1,4096]{2,1,0:T(1,128)} reshape(s32[512,4,8]{2,1,0:T(4,128)S(1)} %copy.21) | data formatting | bytes 131072
  3.7 4.2 %all-to-all-start = ((s32[4,1,4096]{2,1,0:T(1,128)}), s32[4,1,4096]{2,1,0:T(1,128)S(1)}, u32[]{:S(2)}, u32[]{:S(2)}) async-start(s32[4,1,4096]{2,1,0:T(1,128)} %reshape.32), calls=%async_computation | async-start | bytes 131072 | tf_op jit(solution)/shard_map/all_to_all | solution.py:22
  8.0 0.0 copy-done.2
  8.0 0.1 copy.23
  8.1 0.0 copy-done
  8.1 0.3 divide_convert_fusion
  8.4 0.4 copy.27
  8.8 3.3 %all-to-all-done = s32[4,1,4096]{2,1,0:T(1,128)S(1)} async-done(((s32[4,1,4096]{2,1,0:T(1,128)}), s32[4,1,4096]{2,1,0:T(1,128)S(1)}, u32[]{:S(2)}, u32[]{:S(2)}) %all-to-all-start) | async-done | bytes 65568 | tf_op jit(solution)/shard_map/all_to_all | solution.py:22
  12.1 0.5 broadcast.11
  12.6 0.8 %reduce.1 = s32[4,4096]{1,0:T(4,128)S(1)} reduce(s32[4,1,4096]{2,1,0:T(1,128)S(1)} %all-to-all-done, s32[]{:T(128)} %broadcast.11), dimensions={1}, to_apply=%all_to_all.15.reduce_sub_computation | reduce | bytes 131076 | tf_op jit(solution)/shard_map/all_to_all | solution.py:22
  13.4 1.3 %reshape.33 = s32[512,4,8]{2,1,0:T(4,128)S(1)} reshape(s32[4,4096]{1,0:T(4,128)S(1)} %reduce.1) | data formatting | bytes 131072
  14.7 0.3 copy.22
  15.0 0.0 copy-start.4
  15.0 0.4 convert_reduce_fusion
  15.4 0.0 copy-start.3
  15.4 0.2 fusion
  15.7 6.3 %all_to_all.22 = bf16[4,16,256]{2,1,0:T(8,128)(2,1)S(1)} all-to-all(bf16[4,16,256]{2,1,0:T(8,128)(2,1)S(1)} %fusion), channel_id=1, replica_groups=mesh['grp'=8,'lane'=4] {'lane'}, dimensions={0} | all-to-all | bytes 65536 | tf_op jit(solution)/shard_map/all_to_all | solution.py:32
  22.0 0.6 reshape.29
  22.6 6.3 %all-to-all-start.2 = ((bf16[8,2,256]{2,1,0:T(2,128)(2,1)}), bf16[8,2,256]{2,1,0:T(2,128)(2,1)S(1)}, u32[]{:S(2)}, u32[]{:S(2)}) async-start(bf16[8,2,256]{2,1,0:T(2,128)(2,1)} %reshape.29), calls=%async_computation.2 | async-start | bytes 16384 | tf_op jit(solution)/shard_map/all_to_all | solution.py:35
  28.9 0.0 copy-done.4
  28.9 0.1 copy.20
  29.0 0.1 eq.29
  29.1 6.4 %all-to-all-done.2 = bf16[8,2,256]{2,1,0:T(2,128)(2,1)S(1)} async-done(((bf16[8,2,256]{2,1,0:T(2,128)(2,1)}), bf16[8,2,256]{2,1,0:T(2,128)(2,1)S(1)}, u32[]{:S(2)}, u32[]{:S(2)}) %all-to-all-start.2) | async-done | bytes 8224 | tf_op jit(solution)/shard_map/all_to_all | solution.py:35
  35.4 0.4 multiply_reduce_fusion
  35.8 0.6 multiply_reduce_fusion.1
  37.1 38.2 %psum.7 = f32[]{:T(128)} all-reduce(f32[]{:T(128)S(6)} %mul.30), channel_id=1, replica_groups=mesh['grp'=8,'lane'=4] {'grp','lane'}, use_global_device_ids=true, to_apply=%region_4.0 | all-reduce | flops 1 | bytes 8 | tf_op jit(solution)/shard_map/psum | solution.py:44
  76.0 0.0 copy-done.3
  76.0 0.6 sqrt_add_fusion
  76.6 0.0 copy-start.1
  76.6 0.1 broadcast_multiply_fusion
  76.7 1.1 %copy-done.1 = f32[4,256,256]{2,1,0:T(8,128)S(1)} copy-done((f32[4,256,256]{2,1,0:T(8,128)S(1)}, f32[4,256,256]{2,1,0:T(8,128)}, u32[]{:S(2)}) %copy-start.1) | copy-done | bytes 1048600
  77.9 1.2 %divide_subtract_fusion = f32[4,256,256]{2,1,0:T(8,128)} fusion(f32[4,256,256]{2,1,0:T(8,128)S(1)} %copy-done.1, f32[4,256,256]{2,1,0:T(8,128)S(1)} %bitcast.12, f32[4,256]{1,0:T(4,128)S(1)} %get-tuple-element.2), kind=kLoop, calls=%fused_computation.3 | loop fusion | flops 524288 | bytes 3149824 | tf_op jit(solution)/shard_map/sub | solution.py:49
  (6 shorter events, 0.1 us)
Async XLA Ops:
  0.6 7.4 %copy-start.2 = (s32[128,16]{0,1:T(8,128)S(1)}, s32[128,16]{0,1:T(8,128)}, u32[]{:S(2)}) copy-start(s32[128,16]{0,1:T(8,128)} %param.7) | copy-start | bytes 24580
  0.6 7.5 %copy-start = (bf16[128,16,256]{2,1,0:T(8,128)(2,1)S(1)}, bf16[128,16,256]{2,1,0:T(8,128)(2,1)}, u32[]{:S(2)}) copy-start(bf16[128,16,256]{2,1,0:T(8,128)(2,1)} %param.6) | copy-start | bytes 3145732
  3.7 8.4 %all-to-all-start = ((s32[4,1,4096]{2,1,0:T(1,128)}), s32[4,1,4096]{2,1,0:T(1,128)S(1)}, u32[]{:S(2)}, u32[]{:S(2)}) async-start(s32[4,1,4096]{2,1,0:T(1,128)} %reshape.32), calls=%async_computation | async-start | bytes 131072 | tf_op jit(solution)/shard_map/all_to_all | solution.py:22
  15.0 13.9 %copy-start.4 = (s32[1,1,8,2]{2,3,1,0:T(2,128)S(1)}, s32[1,1,8,2]{2,3,1,0:T(2,128)}, u32[]{:S(2)}) copy-start(s32[1,1,8,2]{2,3,1,0:T(2,128)} %param.9) | copy-start | bytes 196
  15.4 60.6 %copy-start.3 = (f32[4,256]{1,0:T(4,128)S(1)}, f32[4,256]{1,0:T(4,128)}, u32[]{:S(2)}) copy-start(f32[4,256]{1,0:T(4,128)} %param.11) | copy-start | bytes 12292
  22.6 12.9 %all-to-all-start.2 = ((bf16[8,2,256]{2,1,0:T(2,128)(2,1)}), bf16[8,2,256]{2,1,0:T(2,128)(2,1)S(1)}, u32[]{:S(2)}, u32[]{:S(2)}) async-start(bf16[8,2,256]{2,1,0:T(2,128)(2,1)} %reshape.29), calls=%async_computation.2 | async-start | bytes 16384 | tf_op jit(solution)/shard_map/all_to_all | solution.py:35
  76.6 1.2 %copy-start.1 = (f32[4,256,256]{2,1,0:T(8,128)S(1)}, f32[4,256,256]{2,1,0:T(8,128)}, u32[]{:S(2)}) copy-start(f32[4,256,256]{2,1,0:T(8,128)} %param.10) | copy-start | bytes 3145732
where the time goes:
time: 79.6 us; the launch traced here: 79 us
  blocking collectives  44.5 us (56%)
  starting transfers between devices  10.6 us (13%)
  waiting for transfers between devices  9.65 us (12%)
  local copies, waits for them, and re-layouts  7.56 us (9%)
  other arithmetic  4.03 us (5%)
  between operations  2.13 us (3%)
    psum x1, blocking collectives, per_device(): norm_total = lax.psum(embed_width * jnp.sum(square_mean), ('grp', 'lane'))  38.2 us
    all_to_all x1, waiting for transfers between devices, per_device(): lax.all_to_all(outgoing, 'grp', split_axis=0, concat_axis=0, tiled=True)  6.35 us
    all_to_all x1, starting transfers between devices, per_device(): lax.all_to_all(outgoing, 'grp', split_axis=0, concat_axis=0, tiled=True)  6.33 us
    all_to_all x1, blocking collectives, per_device(): lax.all_to_all(partial_here, 'lane', split_axis=0, concat_axis=0, tiled=T...  6.3 us
    unnamed x14, local copies, waits for them, and re-layouts  5.6 us
    all_to_all x1, starting transfers between devices, per_device(): lax.all_to_all(lookup_slot, 'lane', split_axis=0, concat_axis=1, tiled=True)  4.24 us
    all_to_all x1, waiting for transfers between devices, per_device(): lax.all_to_all(lookup_slot, 'lane', split_axis=0, concat_axis=1, tiled=True)  3.3 us
  transfers between devices with their start and end apart: 2, of which 2 were waited for; matrix products, arithmetic and copies ran while one was open for 1% of the time, Pallas kernels for 0%

commit v1 on v0

--- a/solution.py
+++ b/solution.py
@@ -19,7 +19,10 @@
     scaled = (grad_pooled.astype(jnp.float32) / bag_len.astype(jnp.float32)[:, :, None]).astype(
         jnp.bfloat16
     )
-    own_slots = lax.all_to_all(lookup_slot, "lane", split_axis=0, concat_axis=1, tiled=True)
+    n_dev = lax.axis_size("lane")
+    blocks = jnp.stack(jnp.split(lookup_slot, n_dev, axis=0), axis=0)
+    blocks = lax.all_to_all(blocks, "lane", split_axis=0, concat_axis=0)
+    own_slots = jnp.concatenate(blocks, axis=1)
     slot_marks = jnp.transpose(
         own_slots.reshape(batch_rows, lane_count, tables_here, bag_depth), (1, 0, 2, 3)
     )

time: 79.6 us -> 74.5 us (0.936)
  local copies, waits for them, and re-layouts: 7.56 us -> 2.63 us
  waiting for transfers between devices: 9.65 us -> 7.73 us
  other arithmetic: 4.03 us -> 5.74 us
    unnamed x14 -> x7, local copies, waits for them, and re-layouts: 5.6 us -> 0.68 us
    all_to_all x1, waiting for transfers between devices: 3.3 us -> 1.38 us  [per_device(): blocks = lax.all_to_all(blocks, 'lane', split_axis=0, concat_axis=0)]
    convert_element_type x1, other arithmetic: 0.34 us -> 1.57 us  [per_device(): (grad_pooled.astype(jnp.float32) / bag_len.astype(jnp.float32)[:, :, None...]
    all_to_all x1 -> x0, other arithmetic: 0.81 us -> none  [per_device(): lax.all_to_all(lookup_slot, 'lane', split_axis=0, concat_axis=1, tiled=True)]
    all_to_all x2 -> x0, local copies, waits for them, and re-layouts: 0.8 us -> none  [per_device(): lax.all_to_all(lookup_slot, 'lane', split_axis=0, concat_axis=1, tiled=True)]
  transfers between devices with their start and end apart: 2 -> 2, of which waited for: 2 -> 2; matrix products, arithmetic and copies ran while one was open for 1% -> 4% of each run, Pallas kernels for 0% -> 0%
where the time goes in v1:
time: 74.5 us; the launch traced here: 73.9 us
  blocking collectives  44.5 us (60%)
  starting transfers between devices  10.6 us (14%)
  waiting for transfers between devices  7.73 us (10%)
  other arithmetic  5.74 us (8%)
  local copies, waits for them, and re-layouts  2.63 us (4%)
  between operations  2.1 us (3%)
    psum x1, blocking collectives, per_device(): norm_total = lax.psum(embed_width * jnp.sum(square_mean), ('grp', 'lane'))  38.2 us
    all_to_all x1, waiting for transfers between devices, per_device(): lax.all_to_all(outgoing, 'grp', split_axis=0, concat_axis=0, tiled=True)  6.35 us
    all_to_all x1, starting transfers between devices, per_device(): lax.all_to_all(outgoing, 'grp', split_axis=0, concat_axis=0, tiled=True)  6.33 us
    all_to_all x1, blocking collectives, per_device(): lax.all_to_all(partial_here, 'lane', split_axis=0, concat_axis=0, tiled=T...  6.3 us
    all_to_all x1, starting transfers between devices, per_device(): blocks = lax.all_to_all(blocks, 'lane', split_axis=0, concat_axis=0)  4.24 us
    convert_element_type x1, other arithmetic, per_device(): (grad_pooled.astype(jnp.float32) / bag_len.astype(jnp.float32)[:, :, None...  1.57 us
  transfers between devices with their start and end apart: 2, of which 2 were waited for; matrix products, arithmetic and copies ran while one was open for 4% of the time, Pallas kernels for 0%

profile of v1, /device:TPU:0, one launch (start us, length us, event | category | flops | bytes accessed | tf_op | source)
XLA Modules:
  0.0 73.9 jit_solution(8555533979986851866)
XLA Ops:
  0.6 0.8 %slice_bitcast_fusion.3 = (s32[1,128,4,8]{1,3,2,0:T(8,128)S(1)}, s32[1,128,4,8]{1,3,2,0:T(8,128)S(1)}, s32[1,128,4,8]{1,3,2,0:T(8,128)S(1)}, s32[1,128,4,8]{1,3,2,0:T(8,128)S(1)}) fusion(s32[512,4,8]{0,2,1:T(8,128)} %param.8), kind=kLoop, calls=%fused_computation.16 | loop fusion | bytes 131072 | tf_op jit(solution)/shard_map/stack | solution.py:23
  1.4 0.6 pad_add_fusion
  2.0 4.2 %all-to-all-start = ((s32[4,128,4,8]{1,3,2,0:T(8,128)}), s32[4,128,4,8]{1,3,2,0:T(8,128)S(1)}, u32[]{:S(2)}, u32[]{:S(2)}) async-start(s32[4,128,4,8]{1,3,2,0:T(8,128)} %pad_add_fusion), calls=%async_computation | async-start | bytes 131072 | tf_op jit(solution)/shard_map/all_to_all | solution.py:24
  6.3 0.7 convert_element_type.24
  7.0 0.1 copy.17
  7.1 1.6 %divide_convert_fusion = bf16[128,16,256]{2,1,0:T(8,128)(2,1)S(1)} fusion(bf16[128,16,256]{2,1,0:T(8,128)(2,1)} %param.6, f32[128,16]{1,0:T(8,128)S(1)} %copy.17), kind=kLoop, calls=%fused_computation | loop fusion | flops 1572864 | bytes 2105344 | tf_op jit(solution)/shard_map/convert_element_type | solution.py:19
  8.7 0.4 copy.21
  9.0 0.0 copy-start.2
  9.0 1.4 %all-to-all-done = s32[4,128,4,8]{1,3,2,0:T(8,128)S(1)} async-done(((s32[4,128,4,8]{1,3,2,0:T(8,128)}), s32[4,128,4,8]{1,3,2,0:T(8,128)S(1)}, u32[]{:S(2)}, u32[]{:S(2)}) %all-to-all-start) | async-done | bytes 65568 | tf_op jit(solution)/shard_map/all_to_all | solution.py:24
  10.4 0.4 convert_reduce_fusion
  10.8 0.2 fusion
  11.0 6.3 %all_to_all.15 = bf16[4,16,256]{2,1,0:T(8,128)(2,1)S(1)} all-to-all(bf16[4,16,256]{2,1,0:T(8,128)(2,1)S(1)} %fusion), channel_id=1, replica_groups=mesh['grp'=8,'lane'=4] {'lane'}, dimensions={0} | all-to-all | bytes 65536 | tf_op jit(solution)/shard_map/all_to_all | solution.py:35
  17.3 0.6 reshape.27
  18.0 6.3 %all-to-all-start.2 = ((bf16[8,2,256]{2,1,0:T(2,128)(2,1)}), bf16[8,2,256]{2,1,0:T(2,128)(2,1)S(1)}, u32[]{:S(2)}, u32[]{:S(2)}) async-start(bf16[8,2,256]{2,1,0:T(2,128)(2,1)} %reshape.27), calls=%async_computation.2 | async-start | bytes 16384 | tf_op jit(solution)/shard_map/all_to_all | solution.py:38
  24.3 0.0 copy-done.2
  24.3 0.1 copy.16
  24.4 0.1 eq.29
  24.5 6.4 %all-to-all-done.2 = bf16[8,2,256]{2,1,0:T(2,128)(2,1)S(1)} async-done(((bf16[8,2,256]{2,1,0:T(2,128)(2,1)}), bf16[8,2,256]{2,1,0:T(2,128)(2,1)S(1)}, u32[]{:S(2)}, u32[]{:S(2)}) %all-to-all-start.2) | async-done | bytes 8224 | tf_op jit(solution)/shard_map/all_to_all | solution.py:38
  30.8 0.4 multiply_reduce_fusion
  31.2 0.6 multiply_reduce_fusion.1
  32.5 38.2 %psum.7 = f32[]{:T(128)} all-reduce(f32[]{:T(128)S(6)} %mul.30), channel_id=1, replica_groups=mesh['grp'=8,'lane'=4] {'grp','lane'}, use_global_device_ids=true, to_apply=%region_4.0 | all-reduce | flops 1 | bytes 8 | tf_op jit(solution)/shard_map/psum | solution.py:47
  71.4 0.0 copy-start.1
  71.4 0.0 copy-start
  71.4 0.1 broadcast_multiply_fusion
  71.5 0.6 copy-done.1
  72.1 0.6 sqrt_add_fusion
  72.7 0.0 copy-done
  72.7 1.2 %divide_subtract_fusion = f32[4,256,256]{2,1,0:T(8,128)} fusion(f32[4,256,256]{2,1,0:T(8,128)S(1)} %copy-done, f32[4,256,256]{2,1,0:T(8,128)S(1)} %bitcast.19, f32[4,256]{1,0:T(4,128)S(1)} %get-tuple-element.2), kind=kLoop, calls=%fused_computation.3 | loop fusion | flops 524288 | bytes 3149824 | tf_op jit(solution)/shard_map/sub | solution.py:52
  (5 shorter events, 0.1 us)
Async XLA Ops:
  2.0 8.4 %all-to-all-start = ((s32[4,128,4,8]{1,3,2,0:T(8,128)}), s32[4,128,4,8]{1,3,2,0:T(8,128)S(1)}, u32[]{:S(2)}, u32[]{:S(2)}) async-start(s32[4,128,4,8]{1,3,2,0:T(8,128)} %pad_add_fusion), calls=%async_computation | async-start | bytes 131072 | tf_op jit(solution)/shard_map/all_to_all | solution.py:24
  9.0 15.3 %copy-start.2 = (s32[1,1,8,2]{2,3,1,0:T(2,128)S(1)}, s32[1,1,8,2]{2,3,1,0:T(2,128)}, u32[]{:S(2)}) copy-start(s32[1,1,8,2]{2,3,1,0:T(2,128)} %param.9) | copy-start | bytes 196
  18.0 12.9 %all-to-all-start.2 = ((bf16[8,2,256]{2,1,0:T(2,128)(2,1)}), bf16[8,2,256]{2,1,0:T(2,128)(2,1)S(1)}, u32[]{:S(2)}, u32[]{:S(2)}) async-start(bf16[8,2,256]{2,1,0:T(2,128)(2,1)} %reshape.27), calls=%async_computation.2 | async-start | bytes 16384 | tf_op jit(solution)/shard_map/all_to_all | solution.py:38
  71.4 0.7 copy-start.1
  71.4 1.3 %copy-start = (f32[4,256,256]{2,1,0:T(8,128)S(1)}, f32[4,256,256]{2,1,0:T(8,128)}, u32[]{:S(2)}) copy-start(f32[4,256,256]{2,1,0:T(8,128)} %param.10) | copy-start | bytes 3145732
